TPU v7x, 256 devices: a whole 4x4x8 slice. The times are simulated.
256 devices in a mesh: section: 8 (over y, core), replica: 32 (over z, x).
Axes of the slice: x: 4, y: 4, z: 8, core: 2. Of those that a mesh axis runs over, the one named last changes fastest.
Arguments:
- gradient: bfloat16 [1024, 131072], P('section', 'replica'), may hold values from -1300 to 1300
- residual: float32 [1024, 131072], P('section', 'replica'), may hold values from -6 to 6
- block_ids: int32 [8, 256], P('section', 'replica'), may hold values from 0 to 15, as said below
- block_counts: int32 [8, 32], P('section', 'replica'), may hold values from 1 to 8, as said below
Outputs:
- new_residual: float32 [1024, 131072], P('section', 'replica')
- update: bfloat16 [1024, 4096], P('section', 'replica')
Inputs may be any that keep to these rules, and one draw needn't show every extreme that they name: `block_ids`: each device's 8 block numbers are distinct; only the first block_counts of them are selected. `block_counts`: in every section some replica selects exactly 8 blocks; the others select at most 4.
All inputs are finite; a program needn't handle non-finite values.
Results may differ from a plain program's by a relative error of at most 0.013.
Values may be sent and summed in bfloat16 or wider, within the bound.
No kernel may reach another device: no remote copies, remote signals or barrier semaphores. Data moves between devices by JAX's collectives and lax.ppermute only.
A program may use at most 64 MiB of HBM per device.

v0:
```python
import jax
import jax.numpy as jnp
from jax import lax
from jax.sharding import Mesh
from jax.sharding import PartitionSpec as P

BLK = 8
REPLICA = ("replica_0", "replica_1")
SECTION = ("section_0", "section_1")


scale_level = 1.0
epsilon = 1e-06


def gathered_by_axis(x, axes, dim):
    if not axes:
        return x
    nearer = lax.all_gather(x, axes[-1], axis=dim, tiled=True)
    return gathered_by_axis(nearer, axes[:-1], dim)


def sent_to_all(x, axis):
    copies = jnp.broadcast_to(x, (lax.axis_size(axis), *x.shape))
    return lax.all_to_all(copies, axis, split_axis=0, concat_axis=0, tiled=True)


def of_everyone(x, axis):
    return sent_to_all(x, axis).sum(axis=0)


def by_axis(x, axes):
    far, near = axes
    return of_everyone(of_everyone(x, near), far)


def deposit(packed, owners, block_total):
    one_hot = (owners[:, None] == jnp.arange(block_total, dtype=jnp.int32)[None, :]).astype(
        jnp.bfloat16
    )
    return jnp.einsum("kb,kxc->bxc", one_hot, packed, preferred_element_type=jnp.float32)


def per_device(gradient, residual, block_ids, block_counts):
    row_count, width = gradient.shape
    replicas = lax.axis_size(REPLICA)
    col_count = width // replicas
    block_total = row_count // BLK
    slot_count = block_ids.shape[1]
    accumulated = gradient.astype(jnp.float32) + residual
    slot_ids = block_ids[0]
    live_slot = jnp.arange(slot_count, dtype=jnp.int32) < block_counts[0, 0]
    hit_table = (
        slot_ids[:, None] == jnp.arange(block_total, dtype=jnp.int32)[None, :]
    ) & live_slot[:, None]
    chosen = jnp.any(hit_table, axis=0)
    row_chosen = jnp.repeat(chosen, BLK)[:, None]
    sent = jnp.where(
        row_chosen, accumulated.astype(jnp.bfloat16).astype(jnp.float32), jnp.float32(0.0)
    )
    new_residual = accumulated - sent
    picked = accumulated.reshape(block_total, BLK, width)[slot_ids]
    packed_blocks = jnp.where(live_slot[:, None, None], picked, jnp.float32(0.0)).astype(
        jnp.bfloat16
    )
    column_parts = packed_blocks.reshape(slot_count, BLK, replicas, col_count)
    received = lax.all_to_all(column_parts, REPLICA, split_axis=2, concat_axis=0, tiled=True)
    owners = gathered_by_axis(slot_ids, REPLICA, 0)
    flat_received = received.reshape(replicas * slot_count, BLK, col_count)
    summed = deposit(flat_received, owners, block_total).reshape(row_count, col_count)
    local_square = jnp.sum(summed * summed)
    norm_total = by_axis(local_square, ("section_0", ("section_1", "replica_0", "replica_1")))
    element_count = lax.axis_size(SECTION) * row_count * width
    root_mean = jnp.sqrt(norm_total / element_count + epsilon)
    clip_factor = scale_level / root_mean
    update = (summed * clip_factor).astype(jnp.bfloat16)
    return (new_residual, update)


def solution(mesh):
    split = Mesh(
        mesh.devices.reshape(4, 2, 8, 4), ("section_0", "section_1", "replica_0", "replica_1")
    )
    return jax.shard_map(
        per_device,
        mesh=split,
        in_specs=(
            P(SECTION, REPLICA),
            P(SECTION, REPLICA),
            P(SECTION, REPLICA),
            P(SECTION, REPLICA),
        ),
        out_specs=(P(SECTION, REPLICA), P(SECTION, REPLICA)),
        check_vma=False,
    )
```

profile of v0, /device:TPU:1, one launch (start us, length us, event | category | flops | bytes accessed | tf_op | source)
XLA Modules:
  0.0 75.2 jit_solution(2620851719656784843)
XLA Ops:
  1.3 0.7 fusion.10
  2.0 2.1 %fusion.1 = bf16[16,8,4096]{2,1,0:T(8,128)(2,1)S(1)} fusion(f32[128,4096]{1,0:T(8,128)} %param.5, bf16[128,4096]{1,0:T(8,128)(2,1)} %param.4), kind=kLoop, calls=%fused_computation.5 | loop fusion | flops 1572864 | bytes 4194304 | tf_op jit(solution)/shard_map/reshape | solution.py:62
  4.0 0.0 copy-start.4
  4.0 0.0 copy-start.3
  4.1 0.0 copy-start.2
  4.1 1.4 %gather_fusion = bf16[8,8,4096]{2,1,0:T(8,128)(2,1)} fusion(bf16[16,8,4096]{2,1,0:T(8,128)(2,1)S(1)} %fusion.1, s32[1024]{0:T(1024)S(1)} %pad_clamp_fusion), kind=kCustom, calls=%fused_computation | custom fusion | bytes 1048608 | tf_op jit(solution)/shard_map/gather | solution.py:62
  5.4 1.4 %fusion = bf16[8,8,32,128]{3,2,1,0:T(8,128)(2,1)S(1)} fusion(bf16[8,8,32,128]{3,1,2,0:T(8,128)(2,1)} %bitcast.35, pred[8]{0:T(512)(128)(4,1)S(1)} %iota_compare_fusion.2), kind=kLoop, calls=%fused_computation.4 | loop fusion | flops 262144 | bytes 1048584 | tf_op jit(solution)/shard_map/convert_element_type | solution.py:63
  6.8 1.0 %copy.14 = bf16[8,8,32,128]{3,1,0,2:T(8,128)(2,1)} copy(bf16[8,8,32,128]{3,2,1,0:T(8,128)(2,1)S(1)} %fusion) | data formatting | bytes 1048576 | tf_op jit(solution)/shard_map/convert_element_type | solution.py:63
  7.8 12.0 %all-to-all-start = ((bf16[8,8,32,128]{3,1,0,2:T(8,128)(2,1)}), bf16[8,8,32,128]{3,1,0,2:T(8,128)(2,1)}, u32[]{:S(2)}, u32[]{:S(2)}) async-start(bf16[8,8,32,128]{3,1,0,2:T(8,128)(2,1)} %copy.14), calls=%async_computation | async-start | bytes 1048576 | tf_op jit(solution)/shard_map/all_to_all | solution.py:67
  19.8 0.0 copy-done.4
  19.8 0.7 dynamic-slice.1
  20.5 0.0 copy-done.3
  20.5 0.6 dynamic-slice
  21.1 0.0 copy-done.2
  21.1 0.1 fusion.9
  21.2 0.1 broadcast_in_dim.41
  21.2 0.1 broadcast_in_dim.42
  22.7 0.1 bitcast_dynamic-update-slice_fusion
  22.8 8.0 %all-reduce = s32[32]{0:T(128)S(1)} all-reduce(s32[32]{0:T(128)S(1)} %bitcast_dynamic-update-slice_fusion), channel_id=2, replica_groups=mesh['section_0'=4,'section_1'=2,'replica_0'=8,'replica_1'=4] {'replica_1'}, use_global_device_ids=true, to_apply=%add | all-reduce | flops 32 | bytes 256
  30.8 0.2 dynamic-update-slice.1
  31.0 11.0 %all-reduce.1 = s32[256]{0:T(256)S(1)} all-reduce(s32[256]{0:T(256)S(1)} %dynamic-update-slice.1), channel_id=3, replica_groups=mesh['section_0'=4,'section_1'=2,'replica_0'=8,'replica_1'=4] {'replica_0'}, use_global_device_ids=true, to_apply=%add.1 | all-reduce | flops 256 | bytes 2048
  42.0 0.0 all-to-all-done
  42.0 1.8 %multiply_reduce_fusion = (f32[]{:T(128)}, f32[16,8,128]{2,0,1:T(8,128)S(1)}) fusion(bf16[32,8,8,1,128]{4,2,1,0,3:T(8,128)(2,1)} %bitcast.9, s32[256]{0:T(256)S(1)} %all-reduce.1), kind=kOutput, calls=%fused_computation.10 | convolution fusion | flops 8425471 | bytes 590852 | tf_op jit(solution)/shard_map/kb,kxc->bxc/dot_general | solution.py:41
  43.8 1.3 %broadcast_in_dim.47 = f32[64,1,1]{2,1,0:T(1,128)} broadcast(f32[]{:T(128)} %get-tuple-element.2), dimensions={} | broadcast | bytes 260 | tf_op jit(solution)/shard_map/broadcast_in_dim | solution.py:24
  45.1 9.7 %all-to-all-start.1 = ((f32[64,1,1]{2,1,0:T(1,128)}), f32[64,1,1]{2,1,0:T(1,128)S(1)}, u32[]{:S(2)}, u32[]{:S(2)}) async-start(f32[64,1,1]{2,1,0:T(1,128)} %broadcast_in_dim.47), calls=%async_computation.1 | async-start | bytes 65536 | tf_op jit(solution)/shard_map/all_to_all | solution.py:25
  54.8 1.7 %select_subtract_fusion = f32[128,4096]{1,0:T(8,128)} fusion(f32[128,4096]{1,0:T(8,128)S(1)} %copy-done, bf16[128,4096]{1,0:T(8,128)(2,1)S(1)} %copy-done.1, pred[128]{0:T(512)(128)(4,1)S(1)} %broadcast_in_dim.42), kind=kLoop, calls=%fused_computation.1 | loop fusion | flops 3145728 | bytes 5243008 | tf_op jit(solution)/shard_map/sub | solution.py:61
  56.5 7.4 %all-to-all-done.1 = f32[64,1,1]{2,1,0:T(1,128)S(1)} async-done(((f32[64,1,1]{2,1,0:T(1,128)}), f32[64,1,1]{2,1,0:T(1,128)S(1)}, u32[]{:S(2)}, u32[]{:S(2)}) %all-to-all-start.1) | async-done | bytes 288 | tf_op jit(solution)/shard_map/all_to_all | solution.py:25
  63.8 0.7 reduce_sum.28
  64.5 0.6 broadcast_in_dim.48
  65.1 8.1 %all_to_all.27 = f32[4,1,1]{2,1,0:T(1,128)S(1)} all-to-all(f32[4,1,1]{2,1,0:T(1,128)S(1)} %broadcast_in_dim.48), channel_id=1, replica_groups=mesh['section_0'=4,'section_1'=2,'replica_0'=8,'replica_1'=4] {'section_0'}, dimensions={0} | all-to-all | bytes 32 | tf_op jit(solution)/shard_map/all_to_all | solution.py:25
  73.3 0.6 reduce_sum.29
  74.6 0.6 copy.30
  (9 shorter events, 0.0 us)
Async XLA Ops:
  4.0 15.8 %copy-start.4 = (u32[256]{0:T(256)S(1)}, u32[256]{0:T(256)}, u32[]{:S(2)}) copy-start(u32[256]{0:T(256)} %constant.23) | copy-start | bytes 3076
  4.0 16.5 %copy-start.3 = (u32[256]{0:T(256)S(1)}, u32[256]{0:T(256)}, u32[]{:S(2)}) copy-start(u32[256]{0:T(256)} %constant.18) | copy-start | bytes 3076
  4.1 17.0 %copy-start.2 = (s32[1,8]{1,0:T(1,128)S(1)}, s32[1,8]{1,0:T(1,128)}, u32[]{:S(2)}) copy-start(s32[1,8]{1,0:T(1,128)} %param.6) | copy-start | bytes 100
  5.4 49.3 %copy-start = (f32[128,4096]{1,0:T(8,128)S(1)}, f32[128,4096]{1,0:T(8,128)}, u32[]{:S(2)}) copy-start(f32[128,4096]{1,0:T(8,128)} %param.5) | copy-start | bytes 6291460
  5.4 49.3 %copy-start.1 = (bf16[128,4096]{1,0:T(8,128)(2,1)S(1)}, bf16[128,4096]{1,0:T(8,128)(2,1)}, u32[]{:S(2)}) copy-start(bf16[128,4096]{1,0:T(8,128)(2,1)} %param.4) | copy-start | bytes 3145732
  7.8 34.2 %all-to-all-start = ((bf16[8,8,32,128]{3,1,0,2:T(8,128)(2,1)}), bf16[8,8,32,128]{3,1,0,2:T(8,128)(2,1)}, u32[]{:S(2)}, u32[]{:S(2)}) async-start(bf16[8,8,32,128]{3,1,0,2:T(8,128)(2,1)} %copy.14), calls=%async_computation | async-start | bytes 1048576 | tf_op jit(solution)/shard_map/all_to_all | solution.py:67
  45.1 18.7 %all-to-all-start.1 = ((f32[64,1,1]{2,1,0:T(1,128)}), f32[64,1,1]{2,1,0:T(1,128)S(1)}, u32[]{:S(2)}, u32[]{:S(2)}) async-start(f32[64,1,1]{2,1,0:T(1,128)} %broadcast_in_dim.47), calls=%async_computation.1 | async-start | bytes 65536 | tf_op jit(solution)/shard_map/all_to_all | solution.py:25
where the time goes:
time: 75.6 us; the launch traced here: 75.2 us
  blocking collectives  27.1 us (36%)
  starting transfers between devices  21.7 us (29%)
  waiting for transfers between devices  7.37 us (10%)
  other arithmetic  7.14 us (9%)
  local copies, waits for them, and re-layouts  6.66 us (9%)
  between operations  3.44 us (5%)
  matrix products  1.84 us (2%)
    unnamed x2, blocking collectives  19 us
    all_to_all x1, starting transfers between devices, per_device(): lax.all_to_all(column_parts, REPLICA, split_axis=2, concat_axis=0, tiled=...  12 us
    all_to_all x1, starting transfers between devices, sent_to_all(): return lax.all_to_all(copies, axis, split_axis=0, concat_axis=0, tiled=True)  9.67 us
    all_to_all x1, blocking collectives, sent_to_all(): return lax.all_to_all(copies, axis, split_axis=0, concat_axis=0, tiled=True)  8.12 us
    all_to_all x1, waiting for transfers between devices, sent_to_all(): return lax.all_to_all(copies, axis, split_axis=0, concat_axis=0, tiled=True)  7.37 us
    reshape x1, other arithmetic, per_device(): picked = accumulated.reshape(block_total, BLK, width)[slot_ids]  2.06 us
    broadcast_in_dim x2, local copies, waits for them, and re-layouts, sent_to_all(): copies = jnp.broadcast_to(x, (lax.axis_size(axis), *x.shape))  1.92 us
    dot_general x1, matrix products, deposit(): jnp.einsum('kb,kxc->bxc', one_hot, packed, preferred_element_type=jnp.flo...  1.84 us
  transfers between devices with their start and end apart: 2, of which 1 were waited for; matrix products, arithmetic and copies ran while one was open for 5% of the time, Pallas kernels for 0%

commit v1 on v0

v1 whole, which is shorter than its diff:
```python
import jax
import jax.numpy as jnp
from jax import lax
from jax.experimental import pallas as pl
from jax.experimental.pallas import tpu as pltpu
from jax.sharding import Mesh
from jax.sharding import PartitionSpec as P

BLK = 8
LANES = 128
REPLICA = ("replica_0", "replica_1")
SECTION = ("section_0", "section_1")
CHIPS = ("section_0", "replica_0", "replica_1")

scale_level = 1.0
epsilon = 1e-06


def pack_kernel(ids, counts, gradient, residual, packed, grad_buf, res_buf, grad_sem, res_sem):
    slots = grad_buf.shape[0]
    dests = packed.shape[0]
    copies = []
    for j in range(slots):
        rows = pl.ds(pl.multiple_of(ids[0, j] * BLK, BLK), BLK)
        copies.append(
            (
                pltpu.make_async_copy(gradient.at[rows, :], grad_buf.at[j], grad_sem.at[j]),
                pltpu.make_async_copy(residual.at[rows, :], res_buf.at[j], res_sem.at[j]),
            )
        )
    for pair in copies:
        for copy in pair:
            copy.start()
    lane = lax.broadcasted_iota(jnp.int32, (BLK, LANES), 1)
    slot_of = (lane // BLK) % slots
    code = jnp.full((BLK, LANES), -1, jnp.int32)
    for j in range(slots):
        row = jnp.where(j < counts[0, 0], ids[0, j] * BLK, -2 * LANES)
        code = jnp.where(slot_of == j, row + lane % BLK, code)
    code = jnp.maximum(code, -1).astype(jnp.float32).astype(jnp.bfloat16)
    for d in range(dests):
        packed[d, slots * BLK :, :] = code
    for j, pair in enumerate(copies):
        for copy in pair:
            copy.wait()
        for d in range(dests):
            cols = slice(d * LANES, (d + 1) * LANES)
            total = grad_buf[j, :, cols].astype(jnp.float32) + res_buf[j, :, cols]
            packed[d, j * BLK : (j + 1) * BLK, :] = total.astype(jnp.bfloat16)


def pack(gradient, residual, block_ids, block_counts, replicas):
    width = gradient.shape[1]
    slots = block_ids.shape[1]
    return pl.pallas_call(
        pack_kernel,
        out_shape=jax.ShapeDtypeStruct((replicas, (slots + 1) * BLK, width // replicas), jnp.bfloat16),
        in_specs=[
            pl.BlockSpec(memory_space=pltpu.SMEM),
            pl.BlockSpec(memory_space=pltpu.SMEM),
            pl.BlockSpec(memory_space=pl.ANY),
            pl.BlockSpec(memory_space=pl.ANY),
        ],
        out_specs=pl.BlockSpec(memory_space=pltpu.VMEM),
        scratch_shapes=[
            pltpu.VMEM((slots, BLK, width), gradient.dtype),
            pltpu.VMEM((slots, BLK, width), residual.dtype),
            pltpu.SemaphoreType.DMA((slots,)),
            pltpu.SemaphoreType.DMA((slots,)),
        ],
        name="pack",
    )(block_ids, block_counts, gradient, residual)


def deposit_kernel(received, summed, squares):
    sources, rows, lanes = received.shape
    live = rows - BLK
    total_rows = summed.shape[0]
    low_half = lax.broadcasted_iota(jnp.int32, (BLK, lanes), 1) < live
    sub = lax.broadcasted_iota(jnp.int32, (BLK, lanes), 0)
    row_ids = [(sub + g * BLK).astype(jnp.float32) for g in range(total_rows // BLK)]
    total = jnp.zeros((total_rows, lanes), jnp.float32)
    for s in range(0, sources, 2):
        code = jnp.where(
            low_half,
            received[s, live:, :].astype(jnp.float32),
            received[s + 1, live:, :].astype(jnp.float32),
        )
        one_hot = jnp.concatenate(
            [jnp.where(code == r, jnp.float32(1.0), jnp.float32(0.0)) for r in row_ids], axis=0
        ).astype(jnp.bfloat16)
        block = received[s : s + 2, :live, :].reshape(2 * live, lanes)
        total = total + jnp.dot(one_hot, block, preferred_element_type=jnp.float32)
    summed[...] = total
    squares[...] = jnp.sum((total * total).reshape(total_rows // BLK, BLK, lanes), axis=0)


def deposit(received, row_count):
    lanes = received.shape[2]
    return pl.pallas_call(
        deposit_kernel,
        out_shape=(
            jax.ShapeDtypeStruct((row_count, lanes), jnp.float32),
            jax.ShapeDtypeStruct((BLK, lanes), jnp.float32),
        ),
        in_specs=[pl.BlockSpec(memory_space=pltpu.VMEM)],
        out_specs=(pl.BlockSpec(memory_space=pltpu.VMEM), pl.BlockSpec(memory_space=pltpu.VMEM)),
        name="deposit",
    )(received)


def per_device(gradient, residual, block_ids, block_counts):
    row_count, width = gradient.shape
    replicas = lax.axis_size(REPLICA)
    block_total = row_count // BLK
    packed = pack(gradient, residual, block_ids, block_counts, replicas)
    received = lax.all_to_all(packed, REPLICA, split_axis=0, concat_axis=0, tiled=True)

    slot_ids = block_ids[0]
    live_slot = jnp.arange(slot_ids.shape[0], dtype=jnp.int32) < block_counts[0, 0]
    hit_table = (
        slot_ids[:, None] == jnp.arange(block_total, dtype=jnp.int32)[None, :]
    ) & live_slot[:, None]
    row_chosen = jnp.repeat(jnp.any(hit_table, axis=0), BLK)[:, None]
    accumulated = gradient.astype(jnp.float32) + residual
    sent = jnp.where(
        row_chosen, accumulated.astype(jnp.bfloat16).astype(jnp.float32), jnp.float32(0.0)
    )
    new_residual = accumulated - sent

    summed, squares = deposit(received, row_count)
    squares = squares.sum(axis=0, keepdims=True)
    squares = squares + lax.ppermute(squares, "section_1", [(0, 1), (1, 0)])
    chips = lax.axis_size(CHIPS)
    copies = jnp.broadcast_to(squares[None], (chips, *squares.shape))
    everyone = lax.all_to_all(copies, CHIPS, split_axis=0, concat_axis=0, tiled=True)
    norm_total = jnp.sum(everyone)
    element_count = lax.axis_size(SECTION) * row_count * width
    root_mean = jnp.sqrt(norm_total / element_count + epsilon)
    clip_factor = scale_level / root_mean
    update = (summed * clip_factor).astype(jnp.bfloat16)
    return (new_residual, update)


def solution(mesh):
    split = Mesh(
        mesh.devices.reshape(4, 2, 8, 4), ("section_0", "section_1", "replica_0", "replica_1")
    )
    return jax.shard_map(
        per_device,
        mesh=split,
        in_specs=(
            P(SECTION, REPLICA),
            P(SECTION, REPLICA),
            P(SECTION, REPLICA),
            P(SECTION, REPLICA),
        ),
        out_specs=(P(SECTION, REPLICA), P(SECTION, REPLICA)),
        check_vma=False,
    )
```

time: 75.6 us -> 62.6 us (0.83)
  blocking collectives: 27.1 us -> 0 us
  waiting for transfers between devices: 7.37 us -> 27 us
  local copies, waits for them, and re-layouts: 6.66 us -> 0.84 us
  Pallas kernels: 0 us -> 5.33 us
  other arithmetic: 7.14 us -> 3.7 us
  matrix products: 1.84 us -> 0 us
  starting transfers between devices: 21.7 us -> 23.3 us
  between operations: 3.44 us -> 2.06 us
    all_to_all x2, waiting for transfers between devices: 7.37 us -> 26.4 us  [the longest x1 17.5 us: per_device(): lax.all_to_all(packed, REPLICA, split_axis=0, concat_axis=0, tiled=True)]
    unnamed x2 -> x0, blocking collectives: 19 us -> none
    all_to_all x1 -> x0, blocking collectives: 8.12 us -> none  [sent_to_all(): return lax.all_to_all(copies, axis, split_axis=0, concat_axis=0, tiled=True)]
    pallas_call x0 -> x2, Pallas kernels: none -> 5.33 us  [the longest x1 3.34 us: pack(): pl.pallas_call(pack_kernel, out_shape=jax.ShapeDtypeStruct((replicas, (sl...]
    ppermute x0 -> x1, starting transfers between devices: none -> 2.38 us  [per_device(): squares = squares + lax.ppermute(squares, 'section_1', [(0, 1), (1, 0)])]
    reshape x1 -> x0, other arithmetic: 2.06 us -> none  [per_device(): picked = accumulated.reshape(block_total, BLK, width)[slot_ids]]
    dot_general x1 -> x0, matrix products: 1.84 us -> none  [deposit(): jnp.einsum('kb,kxc->bxc', one_hot, packed, preferred_element_type=jnp.flo...]
    convert_element_type x2 -> x0, local copies, waits for them, and re-layouts: 1.62 us -> none  [the longest x1 1 us: per_device(): jnp.where(live_slot[:, None, None], picked, jnp.float32(0.0))]
  transfers between devices with their start and end apart: 2 -> 3, of which waited for: 1 -> 3; matrix products, arithmetic and copies ran while one was open for 5% -> 3% of each run, Pallas kernels for 0% -> 0%
where the time goes in v1:
time: 62.6 us; the launch traced here: 62.3 us
  waiting for transfers between devices  27 us (43%)
  starting transfers between devices  23.3 us (37%)
  Pallas kernels  5.33 us (9%)
  other arithmetic  3.7 us (6%)
  between operations  2.06 us (3%)
  local copies, waits for them, and re-layouts  0.84 us (1%)
    all_to_all x1, waiting for transfers between devices, per_device(): lax.all_to_all(packed, REPLICA, split_axis=0, concat_axis=0, tiled=True)  17.5 us
    all_to_all x1, starting transfers between devices, per_device(): lax.all_to_all(packed, REPLICA, split_axis=0, concat_axis=0, tiled=True)  12 us
    all_to_all x1, starting transfers between devices, per_device(): lax.all_to_all(copies, CHIPS, split_axis=0, concat_axis=0, tiled=True)  8.99 us
    all_to_all x1, waiting for transfers between devices, per_device(): lax.all_to_all(copies, CHIPS, split_axis=0, concat_axis=0, tiled=True)  8.87 us
    pallas_call x1, Pallas kernels, pack(): pl.pallas_call(pack_kernel, out_shape=jax.ShapeDtypeStruct((replicas, (sl...  3.34 us
    ppermute x1, starting transfers between devices, per_device(): squares = squares + lax.ppermute(squares, 'section_1', [(0, 1), (1, 0)])  2.38 us
    pallas_call x1, Pallas kernels, deposit(): pl.pallas_call(deposit_kernel, out_shape=(jax.ShapeDtypeStruct((row_count...  1.98 us
    sub x1, other arithmetic, per_device(): new_residual = accumulated - sent  1.67 us
  transfers between devices with their start and end apart: 3, of which 3 were waited for; matrix products, arithmetic and copies ran while one was open for 3% of the time, Pallas kernels for 0%

profile of v1, /device:TPU:1, one launch (start us, length us, event | category | flops | bytes accessed | tf_op | source)
XLA Modules:
  0.0 62.3 jit_solution(5980211957624914149)
XLA Ops:
  1.3 0.0 copy-start.3
  1.3 0.0 copy-start
  1.3 0.0 copy-start.1
  1.3 3.3 %pack.1 = bf16[32,72,128]{2,1,0:T(8,128)(2,1)} custom-call(s32[1,8]{1,0:T(1,128)} %ids.1, s32[1,1]{1,0:T(1,128)} %copy.7.counts, bf16[128,4096]{1,0:T(8,128)(2,1)} %gradient.1, f32[128,4096]{1,0:T(8,128)} %residual.1), custom_call_target="tpu_custom_call" | custom-call | tf_op jit(solution)/shard_map/pack/pallas_call | solution.py:55
  4.7 12.0 %all-to-all-start = ((bf16[32,72,128]{2,1,0:T(8,128)(2,1)}), bf16[32,72,128]{2,1,0:T(8,128)(2,1)}, u32[]{:S(2)}, u32[]{:S(2)}) async-start(bf16[32,72,128]{2,1,0:T(8,128)(2,1)} %pack.1), calls=%async_computation | async-start | bytes 1179648 | tf_op jit(solution)/shard_map/all_to_all | solution.py:117
  16.7 17.5 %all-to-all-done.received = bf16[32,72,128]{2,1,0:T(8,128)(2,1)} async-done(((bf16[32,72,128]{2,1,0:T(8,128)(2,1)}), bf16[32,72,128]{2,1,0:T(8,128)(2,1)}, u32[]{:S(2)}, u32[]{:S(2)}) %all-to-all-start) | async-done | bytes 589856 | tf_op jit(solution)/shard_map/all_to_all | solution.py:117
  34.2 2.0 %deposit.1 = (f32[128,128]{1,0:T(8,128)}, f32[8,128]{1,0:T(8,128)}) custom-call(bf16[32,72,128]{2,1,0:T(8,128)(2,1)} %all-to-all-done.received), custom_call_target="tpu_custom_call" | custom-call | tf_op jit(solution)/shard_map/deposit/pallas_call | solution.py:100
  36.2 0.7 %reduce_sum.18 = f32[128]{0:T(128)S(1)} reduce(f32[8,128]{1,0:T(8,128)} %get-tuple-element.5, f32[]{:T(128)} %constant.1.clone.1), dimensions={0}, to_apply=%region_1.2 | reduce | flops 896 | bytes 4612 | tf_op jit(solution)/shard_map/reduce_sum | solution.py:132
  36.9 2.4 %collective-permute-start = (f32[1,128]{1,0:T(1,128)S(1)}, f32[1,128]{1,0:T(1,128)S(1)}, u32[]{:S(2)}, u32[]{:S(2)}) collective-permute-start(f32[1,128]{1,0:T(1,128)S(1)} %bitcast.10), channel_id=1, source_target_pairs={{0,32},{32,0},{1,33},{33,1},{2,34},{34,2},{3,35},{35,3},{4,36},{36... | collective-permute-start | bytes 1544 | tf_op jit(solution)/shard_map/ppermute | solution.py:133
  39.3 0.0 copy-done.3
  39.3 0.1 fusion.2
  39.4 0.1 broadcast_in_dim.30
  39.4 0.1 broadcast_in_dim.31
  39.5 0.6 collective-permute-done
  40.1 0.6 %broadcast_in_dim.36 = f32[128,1,128]{2,1,0:T(1,128)} broadcast(f32[128]{0:T(128)S(1)} %add_bitcast_fusion), dimensions={2} | broadcast | bytes 66048 | tf_op jit(solution)/shard_map/broadcast_in_dim | solution.py:135
  40.7 9.0 %all-to-all-start.1 = ((f32[128,1,128]{2,1,0:T(1,128)}), f32[128,1,128]{2,1,0:T(1,128)S(1)}, u32[]{:S(2)}, u32[]{:S(2)}) async-start(f32[128,1,128]{2,1,0:T(1,128)} %broadcast_in_dim.36), calls=%async_computation.1 | async-start | bytes 131072 | tf_op jit(solution)/shard_map/all_to_all | solution.py:136
  49.7 0.0 copy-done
  49.8 0.0 copy-done.1
  49.8 0.0 copy-start.2
  49.8 1.7 %select_subtract_fusion = f32[128,4096]{1,0:T(8,128)} fusion(f32[128,4096]{1,0:T(8,128)S(1)} %copy-done, bf16[128,4096]{1,0:T(8,128)(2,1)S(1)} %copy-done.1, pred[128]{0:T(512)(128)(4,1)S(1)} %broadcast_in_dim.31), kind=kLoop, calls=%fused_computation | loop fusion | flops 3145728 | bytes 5243008 | tf_op jit(solution)/shard_map/sub | solution.py:129
  51.4 8.9 %all-to-all-done.1 = f32[128,1,128]{2,1,0:T(1,128)S(1)} async-done(((f32[128,1,128]{2,1,0:T(1,128)}), f32[128,1,128]{2,1,0:T(1,128)S(1)}, u32[]{:S(2)}, u32[]{:S(2)}) %all-to-all-start.1) | async-done | bytes 65568 | tf_op jit(solution)/shard_map/all_to_all | solution.py:136
  60.3 0.6 reduce_sum.19
  61.6 0.0 copy-done.2
  61.6 0.6 multiply_convert_fusion
  (2 shorter events, 0.0 us)
Async XLA Ops:
  1.3 38.0 %copy-start.3 = (s32[1,8]{1,0:T(1,128)S(1)}, s32[1,8]{1,0:T(1,128)}, u32[]{:S(2)}) copy-start(s32[1,8]{1,0:T(1,128)} %ids.1) | copy-start | bytes 100
  1.3 48.5 %copy-start = (f32[128,4096]{1,0:T(8,128)S(1)}, f32[128,4096]{1,0:T(8,128)}, u32[]{:S(2)}) copy-start(f32[128,4096]{1,0:T(8,128)} %residual.1) | copy-start | bytes 6291460
  1.3 48.5 %copy-start.1 = (bf16[128,4096]{1,0:T(8,128)(2,1)S(1)}, bf16[128,4096]{1,0:T(8,128)(2,1)}, u32[]{:S(2)}) copy-start(bf16[128,4096]{1,0:T(8,128)(2,1)} %gradient.1) | copy-start | bytes 3145732
  4.7 29.5 %all-to-all-start = ((bf16[32,72,128]{2,1,0:T(8,128)(2,1)}), bf16[32,72,128]{2,1,0:T(8,128)(2,1)}, u32[]{:S(2)}, u32[]{:S(2)}) async-start(bf16[32,72,128]{2,1,0:T(8,128)(2,1)} %pack.1), calls=%async_computation | async-start | bytes 1179648 | tf_op jit(solution)/shard_map/all_to_all | solution.py:117
  36.9 3.2 %collective-permute-start = (f32[1,128]{1,0:T(1,128)S(1)}, f32[1,128]{1,0:T(1,128)S(1)}, u32[]{:S(2)}, u32[]{:S(2)}) collective-permute-start(f32[1,128]{1,0:T(1,128)S(1)} %bitcast.10), channel_id=1, source_target_pairs={{0,32},{32,0},{1,33},{33,1},{2,34},{34,2},{3,35},{35,3},{4,36},{36... | collective-permute-start | bytes 1544 | tf_op jit(solution)/shard_map/ppermute | solution.py:133
  40.7 19.6 %all-to-all-start.1 = ((f32[128,1,128]{2,1,0:T(1,128)}), f32[128,1,128]{2,1,0:T(1,128)S(1)}, u32[]{:S(2)}, u32[]{:S(2)}) async-start(f32[128,1,128]{2,1,0:T(1,128)} %broadcast_in_dim.36), calls=%async_computation.1 | async-start | bytes 131072 | tf_op jit(solution)/shard_map/all_to_all | solution.py:136
  49.8 11.9 %copy-start.2 = (f32[128,128]{1,0:T(8,128)S(1)}, f32[128,128]{1,0:T(8,128)}, u32[]{:S(2)}) copy-start(f32[128,128]{1,0:T(8,128)} %get-tuple-element.4) | copy-start | bytes 196612
